TPU v7x, 32 devices: a whole 2x2x4 slice. The times are simulated.
32 devices in a mesh: dp: 1, expert: 32 (over z, y, x, core).
Axes of the slice: x: 2, y: 2, z: 4, core: 2. Of those that a mesh axis runs over, the one named last changes fastest.
Arguments:
- tokens: bfloat16 [8192, 2048], P(('dp', 'expert')), may hold values from -6 to 6
- expert_ranks: int32 [32, 8192], P(None, ('dp', 'expert')), may hold values from 0 to 8191, as said below
- capacity: int32 [32], replicated, may hold values from 64 to 128, as said below
- weight_in: bfloat16 [32, 2048, 8192], P('expert', None, 'dp'), may hold values from -0.125 to 0.125
- weight_out: bfloat16 [32, 8192, 2048], P('expert', 'dp'), may hold values from -0.0625 to 0.0625
- gate_weights: float32 [32, 128], P('expert', 'dp'), may hold values from 0.05 to 1
Outputs:
- combined: bfloat16 [8192, 2048], P(('dp', 'expert'))
Inputs may be any that keep to these rules, and one draw needn't show every extreme that they name: `expert_ranks`: for each expert the ranks are a permutation of 0 to 8191. Of the 256 tokens of one device, at most 8 have rank under 128 for one expert; for an expert of capacity 128, some devices have exactly 8. At least one expert has capacity 128.
All inputs are finite; a program needn't handle non-finite values.
Results may differ from a plain program's by a relative error of at most 0.0053.
Values may be sent and summed in bfloat16 or wider, within the bound.
A program may use at most 128 MiB of HBM per device.

v0:
```python
import jax
import jax.numpy as jnp
from jax import lax
from jax.sharding import PartitionSpec as P

MOST = 8


def on_device(tokens, expert_ranks, capacity, weight_in, weight_out, gate_weights):
    dp_count = lax.axis_size("dp")
    expert_count = lax.axis_size("expert")
    token_count, width = tokens.shape
    slots_all = gate_weights.shape[1] * dp_count
    chosen = expert_ranks < capacity[:, None]
    chosen_int = chosen.astype(jnp.int32)
    counts = jnp.sum(chosen_int, axis=1)
    before = jnp.cumsum(chosen_int, axis=1) - chosen_int
    places = lax.broadcasted_iota(jnp.int32, (expert_count, MOST, token_count), 1)
    pack_table = jnp.logical_and(chosen[:, None, :], before[:, None, :] == places)
    pack_table = pack_table.astype(jnp.bfloat16).reshape(expert_count * MOST, token_count)
    packed = jnp.dot(pack_table, tokens, preferred_element_type=jnp.float32).astype(jnp.bfloat16)
    arrived_rows = lax.all_to_all(
        packed.reshape(expert_count, MOST, width), "expert", split_axis=0, concat_axis=0, tiled=True
    )
    own_expert = lax.axis_index("expert")
    expert_mask = (lax.broadcasted_iota(jnp.int32, (expert_count,), 0) == own_expert).astype(
        jnp.int32
    )
    count_table = lax.all_gather(counts[None, :], ("dp", "expert"), axis=0, tiled=True)
    column = jnp.sum(count_table * expert_mask[None, :], axis=1)
    earlier_sums = jnp.cumsum(column) - column
    row_first = lax.axis_index("dp") * expert_count
    starts = lax.dynamic_slice_in_dim(earlier_sums, row_first, expert_count, 0)
    arrived = lax.dynamic_slice_in_dim(column, row_first, expert_count, 0)
    within = lax.broadcasted_iota(jnp.int32, (expert_count, MOST), 1)
    target = jnp.where(within < arrived[:, None], starts[:, None] + within, -1).reshape(
        expert_count * MOST
    )
    slot_ids = lax.broadcasted_iota(jnp.int32, (expert_count * MOST, slots_all), 1)
    place_table = (target[:, None] == slot_ids).astype(jnp.bfloat16)
    flat_rows = arrived_rows.reshape(expert_count * MOST, width)
    local_rows = lax.dot_general(
        place_table, flat_rows, (((0,), (0,)), ((), ())), preferred_element_type=jnp.float32
    ).astype(jnp.bfloat16)
    first_weight = weight_in[0]
    second_weight = weight_out[0]
    slot_rows = lax.psum(local_rows, "dp").astype(jnp.float32).astype(jnp.bfloat16)
    hidden = jnp.maximum(
        jnp.dot(slot_rows, first_weight, preferred_element_type=jnp.float32), 0.0
    ).astype(jnp.bfloat16)
    out_share = lax.psum_scatter(
        jnp.dot(hidden, second_weight, preferred_element_type=jnp.float32),
        "dp",
        scatter_dimension=0,
        tiled=True,
    )
    scaled = (gate_weights[0][:, None] * out_share).astype(jnp.bfloat16)
    returned = jnp.dot(
        place_table,
        lax.all_gather(scaled, "dp", axis=0, tiled=True),
        preferred_element_type=jnp.float32,
    )
    sent_back = returned.astype(jnp.bfloat16).reshape(expert_count, MOST, width)
    results = lax.all_to_all(sent_back, "expert", split_axis=0, concat_axis=0, tiled=True)
    flat_results = results.reshape(expert_count * MOST, width)
    combined = lax.dot_general(
        pack_table, flat_results, (((0,), (0,)), ((), ())), preferred_element_type=jnp.float32
    )
    return combined.astype(jnp.bfloat16)


def solution(mesh):
    in_specs = (
        P(("dp", "expert"), None),
        P(None, ("dp", "expert")),
        P(),
        P("expert", None, "dp"),
        P("expert", "dp", None),
        P("expert", "dp"),
    )
    out_specs = P(("dp", "expert"), None)
    return jax.shard_map(
        on_device, mesh=mesh, in_specs=in_specs, out_specs=out_specs, check_vma=False
    )
```

profile of v0, /device:TPU:0, one launch (start us, length us, event | category | flops | bytes accessed | tf_op | source)
XLA Modules:
  0.0 114.7 jit_solution(305973781898787885)
XLA Ops:
  0.0 0.1 iota.40
  0.1 1.0 convert_reduce_fusion
  1.1 0.6 reduce-window.18
  1.7 0.2 slice_reduce_fusion
  1.9 0.1 convert_subtract_fusion
  2.0 1.5 %fusion.11 = bf16[32,8,2048]{2,1,0:T(8,128)(2,1)} fusion(bf16[256,2048]{1,0:T(8,128)(2,1)S(1)} %copy-done, s32[256]{0:T(256)S(1)} %iota.40, s32[32,256]{1,0:T(8,128)S(1)} %convert_subtract_fusion, pred[32,256]{1,0:T(8,128)(4,1)S(1)} %get-tuple-element.6), kind=kOutput, calls=%fused_computation.10 | convolution fusion | flops 269090816 | bytes 2139136 | tf_op jit(solution)/shard_map/dot_general | solution.py:21
  3.5 7.3 %all-to-all-start = ((bf16[32,8,2048]{2,1,0:T(8,128)(2,1)}), bf16[32,8,2048]{2,1,0:T(8,128)(2,1)S(1)}, u32[]{:S(2)}, u32[]{:S(2)}) async-start(bf16[32,8,2048]{2,1,0:T(8,128)(2,1)} %fusion.11), calls=%async_computation | async-start | bytes 2097152 | tf_op jit(solution)/shard_map/all_to_all | solution.py:22
  10.8 0.2 dynamic-update-slice
  11.1 46.1 %all-reduce = s32[1024]{0:T(1024)S(1)} all-reduce(s32[1024]{0:T(1024)S(1)} %dynamic-update-slice), channel_id=2, replica_groups=mesh['dp'=1,'expert'=32] {'dp','expert'}, use_global_device_ids=true, to_apply=%add | all-reduce | flops 1024 | bytes 8192
  57.2 0.1 reshape.94
  57.3 0.1 multiply_reduce_fusion
  57.4 0.1 copy.20
  57.5 0.1 reduce-window.20
  57.6 0.1 reduce.1
  57.7 0.1 lt.26
  57.8 0.1 lt.27
  57.9 0.1 add.18
  57.9 0.1 add.19
  58.1 0.4 convolution_convert_fusion.2
  58.5 0.0 copy-start.1
  58.5 23.8 %fusion.16 = bf16[128,2048]{1,0:T(8,128)(2,1)S(1)} fusion(bf16[1,8192,2048]{2,1,0:T(8,128)(2,1)} %param.10, bf16[128,2048]{1,0:T(8,128)(2,1)S(1)} %convolution_convert_fusion.2, bf16[1,2048,8192]{2,1,0:T(8,128)(2,1)} %param.9, f32[128]{0:T(128)} %bitcast.54), kind=kOutput, calls=%fused_computation.14 | convolution fusion | flops 8592556032 | bytes 68157952 | tf_op jit(solution)/shard_map/dot_general | solution.py:52
  82.3 0.5 fusion.12
  82.8 30.5 %all_to_all.10 = bf16[32,8,2048]{2,1,0:T(8,128)(2,1)S(1)} all-to-all(bf16[32,8,2048]{2,1,0:T(8,128)(2,1)S(1)} %fusion.12), channel_id=1, replica_groups=mesh['dp'=1,'expert'=32] {'expert'}, dimensions={0} | all-to-all | bytes 2097152 | tf_op jit(solution)/shard_map/all_to_all | solution.py:64
  113.2 1.5 %fusion.10 = bf16[256,2048]{1,0:T(8,128)(2,1)} fusion(bf16[32,8,2048]{2,1,0:T(8,128)(2,1)S(1)} %all_to_all.10, s32[32,256]{1,0:T(8,128)S(1)} %convert_subtract_fusion, pred[32,256]{1,0:T(8,128)(4,1)S(1)} %get-tuple-element.6), kind=kOutput, calls=%fused_computation.7 | convolution fusion | flops 269090816 | bytes 2138112 | tf_op jit(solution)/shard_map/dot_general | solution.py:66
  (12 shorter events, 0.1 us)
Async XLA Ops:
  0.0 2.0 %copy-start = (bf16[256,2048]{1,0:T(8,128)(2,1)S(1)}, bf16[256,2048]{1,0:T(8,128)(2,1)}, u32[]{:S(2)}) copy-start(bf16[256,2048]{1,0:T(8,128)(2,1)} %param.6) | copy-start | bytes 3145732
  3.5 54.6 %all-to-all-start = ((bf16[32,8,2048]{2,1,0:T(8,128)(2,1)}), bf16[32,8,2048]{2,1,0:T(8,128)(2,1)S(1)}, u32[]{:S(2)}, u32[]{:S(2)}) async-start(bf16[32,8,2048]{2,1,0:T(8,128)(2,1)} %fusion.11), calls=%async_computation | async-start | bytes 2097152 | tf_op jit(solution)/shard_map/all_to_all | solution.py:22
  58.5 56.2 %copy-start.1 = (bf16[256,2048]{1,0:T(8,128)(2,1)S(1)}, bf16[256,2048]{1,0:T(8,128)(2,1)}, u32[]{:S(2)}) copy-start(bf16[256,2048]{1,0:T(8,128)(2,1)} %param.6) | copy-start | bytes 3145732
where the time goes:
time: 115 us
  blocking collectives  76.6 us (67%)
  matrix products  27.6 us (24%)
  starting transfers between devices  7.32 us (6%)
  other arithmetic  2.02 us (2%)
    unnamed x1, blocking collectives  46.1 us
    all_to_all x1, blocking collectives, on_device(): lax.all_to_all(sent_back, 'expert', split_axis=0, concat_axis=0, tiled=True)  30.5 us
    dot_general x1, matrix products, on_device(): jnp.dot(hidden, second_weight, preferred_element_type=jnp.float32)  23.8 us
    all_to_all x1, starting transfers between devices, on_device(): lax.all_to_all(packed.reshape(expert_count, MOST, width), 'expert', split...  7.32 us
  transfers between devices with their start and end apart: 1, of which 0 were waited for; matrix products, arithmetic and copies ran while one was open for 1% of the time, Pallas kernels for 0%

commit v1 on v0

--- a/solution.py
+++ b/solution.py
@@ -1,9 +1,274 @@
 import jax
 import jax.numpy as jnp
 from jax import lax
+from jax.experimental import pallas as pl
+from jax.experimental.pallas import tpu as pltpu
 from jax.sharding import PartitionSpec as P
 
 MOST = 8
+PAIR = 2 * MOST
+CHUNKS = 2
+SLOTS_PER_CHUNK = 3
+MESH = pl.DeviceIdType.MESH
+
+
+def one_hot(condition):
+    return jnp.where(condition, 1.0, 0.0)
+
+
+def fused(
+    tokens, ranks, capacity, gates, weight_in, weight_out, combined,
+    wbuf, send_rows, got_rows, send_back, got_back, acc, hidden, oacc, take_left, take_right,
+    wsem, send_sem, recv_sem, own_sem,
+):
+    n = lax.axis_size("expert")
+    me = lax.axis_index("expert")
+    dp = lax.axis_index("dp")
+    token_count, width = tokens.shape
+    slots = gates.shape[1]
+    rows = n * PAIR
+    half = width // 2
+    part = half // CHUNKS
+    nslots, blocks = wbuf.shape[0], wbuf.shape[1]
+    first_units = 2 * CHUNKS
+    units = 4 * CHUNKS
+
+    def load_unit(u):
+        slot = u % nslots
+        which = u % first_units
+        offset = (which % 2) * half + (which // 2) * part
+
+        def start(j, carry):
+            at = pl.multiple_of(j * part, part)
+            if u < first_units:
+                src = weight_in.at[0, pl.ds(offset, part), pl.ds(at, part)]
+            else:
+                src = weight_out.at[0, pl.ds(at, part), pl.ds(offset, part)]
+            pltpu.make_async_copy(src, wbuf.at[slot, j], wsem.at[u]).start()
+            return carry
+
+        lax.fori_loop(0, blocks, start, 0)
+
+    def wait_unit(u):
+        slot = u % nslots
+        pltpu.make_async_copy(wbuf.at[slot], wbuf.at[slot], wsem.at[u]).wait()
+
+    barrier = pltpu.get_barrier_semaphore()
+
+    def greet(k, carry):
+        peer = lax.rem(me + k, n)
+        pl.semaphore_signal(barrier, inc=1, device_id=(dp, peer), device_id_type=MESH)
+        return carry
+
+    lax.fori_loop(1, n, greet, 0)
+    for u in range(nslots):
+        load_unit(u)
+
+    def columns(c, extra):
+        if extra == 0:
+            return pl.ds(c * part, part)
+        return pl.ds(0, extra + part) if c == 0 else pl.ds(extra + c * part, part)
+
+    def exchange(src, dst, phase, c, extra):
+        cols = columns(c, extra)
+        index = phase * CHUNKS + c
+
+        def send(k, carry):
+            peer = lax.rem(me + k, n)
+            pltpu.make_async_remote_copy(
+                src_ref=src.at[pl.ds(pl.multiple_of(peer * PAIR, PAIR), PAIR), cols],
+                dst_ref=dst.at[pl.ds(pl.multiple_of(me * PAIR, PAIR), PAIR), cols],
+                send_sem=send_sem.at[index],
+                recv_sem=recv_sem.at[index],
+                device_id=(dp, peer),
+                device_id_type=MESH,
+            ).start()
+            return carry
+
+        lax.fori_loop(1, n, send, 0)
+        mine = pl.ds(pl.multiple_of(me * PAIR, PAIR), PAIR)
+        pltpu.make_async_copy(src.at[mine, cols], dst.at[mine, cols], own_sem.at[index]).start()
+
+    def arrive(src, dst, phase, c, extra):
+        cols = columns(c, extra)
+        index = phase * CHUNKS + c
+        mine = pl.ds(pl.multiple_of(me * PAIR, PAIR), PAIR)
+        pltpu.make_async_copy(src.at[mine, cols], dst.at[mine, cols], own_sem.at[index]).wait()
+        most = dst.at[pl.ds(0, (n - 1) * PAIR), cols]
+        pltpu.make_async_copy(most, most, recv_sem.at[index]).wait()
+
+    def left(src, phase, c, extra):
+        most = src.at[pl.ds(0, (n - 1) * PAIR), columns(c, extra)]
+        index = phase * CHUNKS + c
+        pltpu.make_async_copy(most, most, send_sem.at[index]).wait()
+
+    chosen = ranks[...] < capacity[...]
+    chosen_one = one_hot(chosen)
+    t_from = lax.broadcasted_iota(jnp.int32, (token_count, token_count), 0)
+    t_to = lax.broadcasted_iota(jnp.int32, (token_count, token_count), 1)
+    earlier = one_hot(t_from < t_to).astype(jnp.bfloat16)
+    before = jnp.dot(chosen_one.astype(jnp.bfloat16), earlier, preferred_element_type=jnp.float32)
+    code = jnp.where(chosen, jnp.minimum(before, float(MOST)), float(MOST)).astype(jnp.bfloat16)
+    row_of = lax.broadcasted_iota(jnp.int32, (rows, n), 0)
+    expert_of = lax.broadcasted_iota(jnp.int32, (rows, n), 1)
+    first_row = expert_of * PAIR
+    repeat = one_hot(jnp.logical_and(row_of >= first_row, row_of < first_row + PAIR))
+    code_rows = jnp.dot(repeat.astype(jnp.bfloat16), code, preferred_element_type=jnp.float32)
+    row_id = lax.broadcasted_iota(jnp.int32, (rows, token_count), 0)
+    place = jnp.bitwise_and(row_id, MOST - 1).astype(jnp.float32)
+    on_right = jnp.bitwise_and(row_id, MOST) > 0
+    hit = one_hot(code_rows == place)
+    pick_left = jnp.where(on_right, 0.0, hit)
+    pick_right = jnp.where(on_right, hit, 0.0)
+    ones = jnp.ones((token_count, slots), jnp.bfloat16)
+    send_rows[:, pl.ds(0, slots)] = jnp.dot(
+        hit.astype(jnp.bfloat16), ones, preferred_element_type=jnp.float32
+    ).astype(jnp.bfloat16)
+    pick_left_low = pick_left.astype(jnp.bfloat16)
+    pick_right_low = pick_right.astype(jnp.bfloat16)
+    for c in range(CHUNKS):
+        send_rows[:, pl.ds(slots + c * part, part)] = (
+            jnp.dot(
+                pick_left_low, tokens[:, pl.ds(c * part, part)],
+                preferred_element_type=jnp.float32,
+            )
+            + jnp.dot(
+                pick_right_low, tokens[:, pl.ds(half + c * part, part)],
+                preferred_element_type=jnp.float32,
+            )
+        ).astype(jnp.bfloat16)
+        if c == 0:
+            pl.semaphore_wait(barrier, n - 1)
+        exchange(send_rows, got_rows, 0, c, slots)
+    take_left[...] = pick_left.T.astype(jnp.bfloat16)
+    take_right[...] = pick_right.T.astype(jnp.bfloat16)
+    gate_column = jnp.broadcast_to(gates[...], (slots, slots)).T[:, 0:1]
+    r_to = lax.broadcasted_iota(jnp.int32, (rows, rows), 0)
+    r_from = lax.broadcasted_iota(jnp.int32, (rows, rows), 1)
+    base = r_to - jnp.bitwise_and(r_to, MOST)
+    ahead = one_hot(jnp.logical_and(r_from < base, jnp.bitwise_and(r_from, MOST) == 0))
+    ahead = ahead.astype(jnp.bfloat16)
+
+    arrive(send_rows, got_rows, 0, 0, slots)
+    valid = got_rows[:, pl.ds(0, slots)]
+    slot_of = jnp.dot(ahead, valid, preferred_element_type=jnp.float32)
+    slot_id = lax.broadcasted_iota(jnp.int32, (rows, slots), 1).astype(jnp.float32)
+    spot = jnp.where(slot_of == slot_id, valid.astype(jnp.float32), 0.0)
+    right_row = jnp.bitwise_and(lax.broadcasted_iota(jnp.int32, (rows, slots), 0), MOST) > 0
+    put_left = jnp.where(right_row, 0.0, spot)
+    put_right = jnp.where(right_row, spot, 0.0)
+    get_left = put_left.T.astype(jnp.bfloat16)
+    get_right = put_right.T.astype(jnp.bfloat16)
+    put_left = put_left.astype(jnp.bfloat16)
+    put_right = put_right.astype(jnp.bfloat16)
+
+    for c in range(CHUNKS):
+        if c > 0:
+            arrive(send_rows, got_rows, 0, c, slots)
+        here = got_rows[:, pl.ds(slots + c * part, part)]
+        x_left = jnp.dot(get_left, here, preferred_element_type=jnp.float32).astype(jnp.bfloat16)
+        x_right = jnp.dot(get_right, here, preferred_element_type=jnp.float32).astype(jnp.bfloat16)
+        u = 2 * c
+        wait_unit(u)
+        wait_unit(u + 1)
+
+        def first(j, carry):
+            term = jnp.dot(x_left, wbuf[u % nslots, j], preferred_element_type=jnp.float32)
+            term += jnp.dot(x_right, wbuf[(u + 1) % nslots, j], preferred_element_type=jnp.float32)
+            if c > 0:
+                term += acc[j]
+            if c < CHUNKS - 1:
+                acc[j] = term
+            else:
+                hidden[j] = jnp.maximum(term, 0.0).astype(jnp.bfloat16)
+            return carry
+
+        lax.fori_loop(0, blocks, first, 0)
+        for v in (u, u + 1):
+            if v + nslots < units:
+                load_unit(v + nslots)
+
+    for c in range(CHUNKS):
+        u = first_units + 2 * c
+        wait_unit(u)
+        wait_unit(u + 1)
+        oacc[...] = jnp.zeros_like(oacc)
+
+        def second(j, carry):
+            for side in range(2):
+                term = oacc[side]
+                for i in range(2):
+                    term += jnp.dot(
+                        hidden[2 * j + i], wbuf[(u + side) % nslots, 2 * j + i],
+                        preferred_element_type=jnp.float32,
+                    )
+                oacc[side] = term
+            return carry
+
+        lax.fori_loop(0, blocks // 2, second, 0)
+        scaled_left = (gate_column * oacc[0]).astype(jnp.bfloat16)
+        scaled_right = (gate_column * oacc[1]).astype(jnp.bfloat16)
+        send_back[:, pl.ds(c * part, part)] = (
+            jnp.dot(put_left, scaled_left, preferred_element_type=jnp.float32)
+            + jnp.dot(put_right, scaled_right, preferred_element_type=jnp.float32)
+        ).astype(jnp.bfloat16)
+        for v in (u, u + 1):
+            if v + nslots < units:
+                load_unit(v + nslots)
+        exchange(send_back, got_back, 1, c, 0)
+
+    for c in range(CHUNKS):
+        arrive(send_back, got_back, 1, c, 0)
+        here = got_back[:, pl.ds(c * part, part)]
+        combined[:, pl.ds(c * part, part)] = jnp.dot(
+            take_left[...], here, preferred_element_type=jnp.float32
+        ).astype(combined.dtype)
+        combined[:, pl.ds(half + c * part, part)] = jnp.dot(
+            take_right[...], here, preferred_element_type=jnp.float32
+        ).astype(combined.dtype)
+    for c in range(CHUNKS):
+        left(send_rows, 0, c, slots)
+        left(send_back, 1, c, 0)
+
+
+def on_device_fused(tokens, expert_ranks, capacity, weight_in, weight_out, gate_weights):
+    n = lax.axis_size("expert")
+    token_count, width = tokens.shape
+    hidden_units = weight_in.shape[2]
+    slots = gate_weights.shape[1]
+    rows = n * PAIR
+    half = width // 2
+    part = half // CHUNKS
+    blocks = hidden_units // part
+    low, wide = jnp.bfloat16, jnp.float32
+    vmem = pl.BlockSpec(memory_space=pltpu.VMEM)
+    anywhere = pl.BlockSpec(memory_space=pl.ANY)
+    return pl.pallas_call(
+        fused,
+        out_shape=jax.ShapeDtypeStruct((token_count, width), low),
+        in_specs=[vmem, vmem, vmem, vmem, anywhere, anywhere],
+        out_specs=vmem,
+        scratch_shapes=[
+            pltpu.VMEM((SLOTS_PER_CHUNK * CHUNKS, blocks, part, part), low),
+            pltpu.VMEM((rows, slots + half), low),
+            pltpu.VMEM((rows, slots + half), low),
+            pltpu.VMEM((rows, half), low),
+            pltpu.VMEM((rows, half), low),
+            pltpu.VMEM((blocks, slots, part), wide),
+            pltpu.VMEM((blocks, slots, part), low),
+            pltpu.VMEM((2, slots, part), wide),
+            pltpu.VMEM((token_count, rows), low),
+            pltpu.VMEM((token_count, rows), low),
+            pltpu.SemaphoreType.DMA((4 * CHUNKS,)),
+            pltpu.SemaphoreType.DMA((2 * CHUNKS,)),
+            pltpu.SemaphoreType.DMA((2 * CHUNKS,)),
+            pltpu.SemaphoreType.DMA((2 * CHUNKS,)),
+        ],
+        compiler_params=pltpu.CompilerParams(
+            collective_id=0, has_side_effects=True, vmem_limit_bytes=67043328
+        ),
+        name="fused",
+    )(tokens, expert_ranks, capacity[:, None], gate_weights, weight_in, weight_out)
 
 
 def on_device(tokens, expert_ranks, capacity, weight_in, weight_out, gate_weights):
@@ -79,6 +344,7 @@
         P("expert", "dp"),
     )
     out_specs = P(("dp", "expert"), None)
+    one_share = mesh.shape["dp"] == 1
     return jax.shard_map(
-        on_device, mesh=mesh, in_specs=in_specs, out_specs=out_specs, check_vma=False
-    )
+        on_device_fused if one_share else on_device, mesh=mesh, in_specs=in_specs, out_specs=out_specs, check_vma=False
+    )

time: 115 us -> 72 us (0.63)
  the two profiles are of different devices: /device:TPU:0 before, /device:TPU:29 now
where the time goes in v1:
time: 72 us; the launch traced here: 71.8 us
  Pallas kernels  68.1 us (95%)
  local copies, waits for them, and re-layouts  3.64 us (5%)
    pallas_call x1, Pallas kernels, on_device_fused(): pl.pallas_call(fused, out_shape=jax.ShapeDtypeStruct((token_count, width)...  68.1 us
    unnamed x1, local copies, waits for them, and re-layouts  2.3 us

profile of v1, /device:TPU:29, one launch (start us, length us, event | category | flops | bytes accessed | tf_op | source)
XLA Modules:
  0.0 71.8 jit_solution(12437531395142321920)
XLA Ops:
  0.0 1.3 %copy.7.capacity = s32[32,1]{1,0:T(8,128)} copy(s32[32,1]{0,1:T(1,128)} %bitcast.1) | data formatting | bytes 256 | tf_op jit(solution)/shard_map/broadcast_in_dim | solution.py:271
  1.3 68.1 %fused.1 = bf16[256,2048]{1,0:T(8,128)(2,1)} custom-call(bf16[256,2048]{1,0:T(8,128)(2,1)} %tokens.1, s32[32,256]{1,0:T(8,128)} %ranks.1, s32[32,1]{1,0:T(8,128)} %copy.7.capacity, f32[1,128]{1,0:T(1,128)} %gates.1, bf16[1,2048,8192]{2,1,0:T(8,128)(2,1)} %weight_in.1, bf16[1,8192,2048]{2,1,0:T(8,128)(2,1)} %weight_out.1), custom_call_target="tpu_custom_call" | custom-call | tf_op jit(solution)/shard_map/fused/pallas_call | solution.py:246
  69.5 2.3 %copy.9 = bf16[256,2048]{1,0:T(8,128)(2,1)} copy(bf16[256,2048]{1,0:T(8,128)(2,1)} %fused.1) | data formatting | bytes 2097152
